TPU v7x, 32 devices: a whole 2x2x4 slice. The times are simulated.
32 devices in a mesh: occ: 8 (over z, y), ao: 4 (over x, core).
Axes of the slice: x: 2, y: 2, z: 4, core: 2. Of those that a mesh axis runs over, the one named last changes fastest.
Arguments:
- amplitudes: bfloat16 [8, 640, 19456], P(None, 'occ', 'ao'), may hold values from -6 to 6
- occ_coef: bfloat16 [512, 640], P(None, 'occ'), may hold values from -0.25 to 0.25
- vir_coef: bfloat16 [512, 19456], P('occ', 'ao'), may hold values from -0.25 to 0.25
- occ_energy: float32 [640], P('occ'), may hold values from -1.5 to -0.3
- vir_energy: float32 [19456], P('ao'), may hold values from 0.05 to 2.5
- kernel: float32 [512], replicated, may hold values from 2 to 10
Outputs:
- residual: bfloat16 [8, 640, 19456], P(None, 'occ', 'ao')
- projected: float32 [8, 8], replicated
All inputs are finite; a program needn't handle non-finite values.
Results may differ from a plain program's by a relative error of at most 0.0049.
Values may be sent and summed in bfloat16 or wider, within the bound.
A program may use at most 128 MiB of HBM per device.

v0:
```python
import jax
import jax.numpy as jnp
from jax import lax
from jax.sharding import PartitionSpec as P


def shards(amplitudes, occ_coef, vir_coef, occ_energy, vir_energy, kernel):
    trials, occ_dev, vir_dev = amplitudes.shape
    row_total = occ_coef.shape[0]
    flat_amps = amplitudes.reshape(trials * occ_dev, vir_dev)
    occ_trans = occ_coef.T.astype(jnp.float32)
    whole_rows = lax.all_gather(vir_coef, "occ", axis=0, tiled=True)
    row_count = whole_rows.shape[0]
    half_done = lax.dot_general(
        flat_amps, whole_rows, (((1,), (1,)), ((), ())), preferred_element_type=jnp.float32
    )
    half_done = half_done.reshape(trials, occ_dev, row_count)
    partial_value = jnp.sum(half_done * occ_trans[None], axis=1)
    amps_rows = amplitudes.reshape(trials, occ_dev * vir_dev)
    density = lax.psum(partial_value, ("occ", "ao"))
    potential = kernel[None, :] * density
    weighted = (
        (occ_trans[None] * potential[:, None, :])
        .astype(jnp.bfloat16)
        .reshape(trials * occ_dev, row_total)
    )
    coupling = jnp.dot(weighted, whole_rows, preferred_element_type=jnp.float32)
    energy_gaps = vir_energy[None, :] - occ_energy[:, None]
    sigma_block = energy_gaps[None] * amplitudes.astype(jnp.float32) + coupling.reshape(
        trials, occ_dev, vir_dev
    )

    def gram_column(sigma_one):
        return jnp.sum(amplitudes.astype(jnp.float32) * sigma_one[None], axis=(1, 2))

    gram_local = lax.map(gram_column, sigma_block).T
    correlation_local = jnp.dot(amps_rows, amps_rows.T, preferred_element_type=jnp.float32)
    gram, correlation = lax.psum((gram_local, correlation_local), ("occ", "ao"))
    norms = jnp.diagonal(correlation) + 1e-06
    ritz_values = jnp.diagonal(gram) / norms
    residual = (sigma_block - ritz_values[:, None, None] * amplitudes.astype(jnp.float32)).astype(
        jnp.bfloat16
    )
    projected = gram / jnp.sqrt(norms[:, None] * norms[None, :])
    return (residual, projected)


def solution(mesh):
    placed = (P(None, "occ", "ao"), P(None, "occ"), P("occ", "ao"), P("occ"), P("ao"), P())
    return jax.shard_map(
        shards, mesh=mesh, in_specs=placed, out_specs=(P(None, "occ", "ao"), P()), check_vma=False
    )
```

profile of v0, /device:TPU:0, one launch (start us, length us, event | category | flops | bytes accessed | tf_op | source)
XLA Modules:
  0.0 258.6 jit_solution(4018655278099293986)
XLA Ops:
  7.2 0.0 all-gather.2.cloned.1.call-start
  7.2 0.7 all-gather.2.cloned.1.call-update
  7.9 0.9 convert_bitcast_fusion
  8.8 11.1 %fusion.14 = f32[8,8]{1,0:T(8,128)S(1)} fusion(bf16[8,80,4864]{2,1,0:T(8,128)(2,1)} %param.8), kind=kOutput, calls=%fused_computation.17 | convolution fusion | flops 49807360 | bytes 6226176 | tf_op jit(solution)/shard_map/dot_general | solution.py:37
  19.9 0.2 broadcast_subtract_fusion
  20.1 75.4 %all-gather.2.cloned.1.call-done = bf16[512,4864]{1,0:T(8,128)(2,1)} async-done(((bf16[64,4864]{1,0:T(8,128)(2,1)}), bf16[512,4864]{1,0:T(8,128)(2,1)}) %all-gather.2.cloned.1.call-update) | async-done | bytes 4980752 | tf_op jit(solution)/shard_map/all_gather | solution.py:12
  95.5 7.6 %fusion.11 = f32[8,512]{1,0:T(8,128)S(1)} fusion(bf16[8,80,4864]{2,1,0:T(8,128)(2,1)} %param.8, bf16[512,4864]{1,0:T(8,128)(2,1)} %all-gather.2.cloned.1.call-done, f32[80,512]{1,0:T(8,128)S(1)} %convert_bitcast_fusion), kind=kOutput, calls=%fused_computation.16 | convolution fusion | flops 3188322304 | bytes 11386880 | tf_op jit(solution)/shard_map/dot_general | solution.py:14
  103.2 38.8 %psum.21 = f32[8,512]{1,0:T(8,128)S(1)} all-reduce(f32[8,512]{1,0:T(8,128)S(1)} %fusion.11), channel_id=1, replica_groups=mesh['occ'=8,'ao'=4] {'occ','ao'}, use_global_device_ids=true, to_apply=%region_1.0 | all-reduce | flops 4096 | bytes 32768 | tf_op jit(solution)/shard_map/psum | solution.py:20
  142.0 9.7 %fusion = f32[8,80,4864]{2,1,0:T(8,128)} fusion(bf16[8,80,4864]{2,1,0:T(8,128)(2,1)} %param.8, f32[80,4864]{1,0:T(8,128)S(1)} %broadcast_subtract_fusion, bf16[512,4864]{1,0:T(8,128)(2,1)} %all-gather.2.cloned.1.call-done, f32[8,512]{1,0:T(8,128)S(1)} %broadcast_multiply_fusion, f32[80,512]{1,0:T(8,128)S(1)} %convert_bitcast_fusion), kind=kOutput, calls=%fused_computation.6 | convolution fusion | flops 3197665280 | bytes 25395200 | tf_op jit(solution)/shard_map/dot_general | solution.py:27
  151.7 46.7 %while.10 = (s32[]{:T(128)}, f32[8,8]{1,0:T(8,128)S(1)}, bf16[8,80,4864]{2,1,0:T(8,128)(2,1)}, f32[8,80,4864]{2,1,0:T(8,128)}, s32[]{:T(128)}, /*index=5*/s32[]{:T(128)}) while((s32[]{:T(128)}, f32[8,8]{1,0:T(8,128)S(1)}, bf16[8,80,4864]{2,1,0:T(8,128)(2,1)}, f32[8,80,4864]{2,1,0:T(8,128)}, s32[]{:T(128)}, /*index=5*/s32[]{:T(128)}) %tuple.23), condition=%wide.region_4.5_spmd, body=%wide.region_2.4_spmd.sunk | while | flops 9338874 | bytes 10895533 | solution.py:36
  151.7 1.5 dynamic-slice_bitcast_fusion.2
  153.2 4.3 %multiply_reduce_fusion.2 = f32[8]{0:T(128)S(1)} fusion(bf16[8,80,4864]{2,1,0:T(8,128)(2,1)} %get-tuple-element.76, f32[80,4864]{1,0:T(8,128)S(1)} %dynamic-slice_bitcast_fusion.2), kind=kLoop, calls=%fused_computation.2.clone.1 | loop fusion | flops 9338872 | bytes 7782432 | tf_op jit(solution)/shard_map/while/body/eval_jaxpr/reduce_sum | solution.py:34
  157.5 1.5 dynamic-slice_bitcast_fusion.2
  159.0 4.3 %multiply_reduce_fusion.2 = f32[8]{0:T(128)S(1)} fusion(bf16[8,80,4864]{2,1,0:T(8,128)(2,1)} %get-tuple-element.76, f32[80,4864]{1,0:T(8,128)S(1)} %dynamic-slice_bitcast_fusion.2), kind=kLoop, calls=%fused_computation.2.clone.1 | loop fusion | flops 9338872 | bytes 7782432 | tf_op jit(solution)/shard_map/while/body/eval_jaxpr/reduce_sum | solution.py:34
  163.3 1.5 dynamic-slice_bitcast_fusion.2
  164.8 4.3 %multiply_reduce_fusion.2 = f32[8]{0:T(128)S(1)} fusion(bf16[8,80,4864]{2,1,0:T(8,128)(2,1)} %get-tuple-element.76, f32[80,4864]{1,0:T(8,128)S(1)} %dynamic-slice_bitcast_fusion.2), kind=kLoop, calls=%fused_computation.2.clone.1 | loop fusion | flops 9338872 | bytes 7782432 | tf_op jit(solution)/shard_map/while/body/eval_jaxpr/reduce_sum | solution.py:34
  169.2 1.5 dynamic-slice_bitcast_fusion.2
  170.7 4.3 %multiply_reduce_fusion.2 = f32[8]{0:T(128)S(1)} fusion(bf16[8,80,4864]{2,1,0:T(8,128)(2,1)} %get-tuple-element.76, f32[80,4864]{1,0:T(8,128)S(1)} %dynamic-slice_bitcast_fusion.2), kind=kLoop, calls=%fused_computation.2.clone.1 | loop fusion | flops 9338872 | bytes 7782432 | tf_op jit(solution)/shard_map/while/body/eval_jaxpr/reduce_sum | solution.py:34
  175.0 1.5 dynamic-slice_bitcast_fusion.2
  176.5 4.3 %multiply_reduce_fusion.2 = f32[8]{0:T(128)S(1)} fusion(bf16[8,80,4864]{2,1,0:T(8,128)(2,1)} %get-tuple-element.76, f32[80,4864]{1,0:T(8,128)S(1)} %dynamic-slice_bitcast_fusion.2), kind=kLoop, calls=%fused_computation.2.clone.1 | loop fusion | flops 9338872 | bytes 7782432 | tf_op jit(solution)/shard_map/while/body/eval_jaxpr/reduce_sum | solution.py:34
  180.8 1.5 dynamic-slice_bitcast_fusion.2
  182.3 4.3 %multiply_reduce_fusion.2 = f32[8]{0:T(128)S(1)} fusion(bf16[8,80,4864]{2,1,0:T(8,128)(2,1)} %get-tuple-element.76, f32[80,4864]{1,0:T(8,128)S(1)} %dynamic-slice_bitcast_fusion.2), kind=kLoop, calls=%fused_computation.2.clone.1 | loop fusion | flops 9338872 | bytes 7782432 | tf_op jit(solution)/shard_map/while/body/eval_jaxpr/reduce_sum | solution.py:34
  186.7 1.5 dynamic-slice_bitcast_fusion.2
  188.2 4.3 %multiply_reduce_fusion.2 = f32[8]{0:T(128)S(1)} fusion(bf16[8,80,4864]{2,1,0:T(8,128)(2,1)} %get-tuple-element.76, f32[80,4864]{1,0:T(8,128)S(1)} %dynamic-slice_bitcast_fusion.2), kind=kLoop, calls=%fused_computation.2.clone.1 | loop fusion | flops 9338872 | bytes 7782432 | tf_op jit(solution)/shard_map/while/body/eval_jaxpr/reduce_sum | solution.py:34
  192.5 1.5 dynamic-slice_bitcast_fusion.2
  194.0 4.3 %multiply_reduce_fusion.2 = f32[8]{0:T(128)S(1)} fusion(bf16[8,80,4864]{2,1,0:T(8,128)(2,1)} %get-tuple-element.76, f32[80,4864]{1,0:T(8,128)S(1)} %dynamic-slice_bitcast_fusion.2), kind=kLoop, calls=%fused_computation.2.clone.1 | loop fusion | flops 9338872 | bytes 7782432 | tf_op jit(solution)/shard_map/while/body/eval_jaxpr/reduce_sum | solution.py:34
  198.3 0.1 copy.11
  198.4 40.7 %all-reduce = (f32[8,8]{1,0:T(8,128)S(1)}, f32[8,8]{1,0:T(8,128)S(1)}) all-reduce(f32[8,8]{1,0:T(8,128)S(1)} %bitcast.25, f32[8,8]{1,0:T(8,128)S(1)} %fusion.14), channel_id=1, replica_groups=mesh['occ'=8,'ao'=4] {'occ','ao'}, use_global_device_ids=true, to_apply=%region_5.6 | all-reduce | flops 128 | bytes 1024 | tf_op jit(solution)/shard_map/psum | solution.py:38
  239.1 0.6 gather_fusion
  239.7 0.6 gather_fusion.1
  240.4 0.7 rsqrt_multiply_fusion
  241.0 10.8 %fusion.2 = bf16[8,80,4864]{2,1,0:T(8,128)(2,1)} fusion(f32[8,80,4864]{2,1,0:T(8,128)} %get-tuple-element.82, bf16[8,80,4864]{2,1,0:T(8,128)(2,1)} %get-tuple-element.81, f32[8]{0:T(128)S(1)} %get-tuple-element.36), kind=kLoop, calls=%fused_computation.8 | loop fusion | flops 12451840 | bytes 24903712 | tf_op jit(solution)/shard_map/convert_element_type | solution.py:41
  (18 shorter events, 0.2 us)
Async XLA Ops:
  7.2 12.8 %copy-start.2 = (f32[80]{0:T(128)S(1)}, f32[80]{0:T(128)}, u32[]{:S(2)}) copy-start(f32[80]{0:T(128)} %param.11) | copy-start | bytes 964
  7.2 12.8 %copy-start = (f32[4864]{0:T(1024)S(1)}, f32[4864]{0:T(1024)}, u32[]{:S(2)}) copy-start(f32[4864]{0:T(1024)} %param.12) | copy-start | bytes 58372
  7.2 88.4 %all-gather.2.cloned.1.call-start = ((), (), s32[]{:S(2)}) async-start(), calls=%async_computation | async-start | bytes 5603328 | tf_op jit(solution)/shard_map/all_gather | solution.py:12
  20.1 121.8 %copy-start.1 = (f32[512]{0:T(512)S(1)}, f32[512]{0:T(512)}, u32[]{:S(2)}) copy-start(f32[512]{0:T(512)} %param.13) | copy-start | bytes 6148
Sparse Core Ops, SparseCore 0:
  10.2 85.3 all-gather.1
where the time goes:
time: 259 us
  blocking collectives  79.5 us (31%)
  waiting for transfers between devices  76.1 us (29%)
  other arithmetic  46.9 us (18%)
  matrix products  28.4 us (11%)
  between operations  14.1 us (5%)
  local copies, waits for them, and re-layouts  13.6 us (5%)
    all_gather x1, waiting for transfers between devices, shards(): whole_rows = lax.all_gather(vir_coef, 'occ', axis=0, tiled=True)  75.4 us
    psum x1, blocking collectives, shards(): gram, correlation = lax.psum((gram_local, correlation_local), ('occ', 'ao'))  40.7 us
    psum x1, blocking collectives, shards(): density = lax.psum(partial_value, ('occ', 'ao'))  38.8 us
    reduce_sum x8, other arithmetic, gram_column(): jnp.sum(amplitudes.astype(jnp.float32) * sigma_one[None], axis=(1, 2))  34.4 us
    mul x8, local copies, waits for them, and re-layouts, gram_column(): amplitudes.astype(jnp.float32) * sigma_one[None]  12.1 us
    dot_general x1, matrix products, shards(): jnp.dot(amps_rows, amps_rows.T, preferred_element_type=jnp.float32)  11.1 us
    convert_element_type x1, other arithmetic, shards(): (sigma_block - ritz_values[:, None, None] * amplitudes.astype(jnp.float32...  10.8 us
    dot_general x1, matrix products, shards(): coupling = jnp.dot(weighted, whole_rows, preferred_element_type=jnp.float32)  9.7 us
  transfers between devices with their start and end apart: 1, of which 1 were waited for; matrix products, arithmetic and copies ran while one was open for 5% of the time, Pallas kernels for 0%

commit v1 on v0

--- a/solution.py
+++ b/solution.py
@@ -17,7 +17,7 @@
     half_done = half_done.reshape(trials, occ_dev, row_count)
     partial_value = jnp.sum(half_done * occ_trans[None], axis=1)
     amps_rows = amplitudes.reshape(trials, occ_dev * vir_dev)
-    density = lax.psum(partial_value, ("occ", "ao"))
+    density = lax.psum(lax.psum(partial_value, "ao"), "occ")
     potential = kernel[None, :] * density
     weighted = (
         (occ_trans[None] * potential[:, None, :])

time: 259 us -> 263 us (1.015)
  blocking collectives: 79.5 us -> 82.5 us
    psum x1 -> x2, blocking collectives: 38.8 us -> 45.6 us  [shards(): density = lax.psum(lax.psum(partial_value, 'ao'), 'occ')]
    psum x1, blocking collectives: 40.7 us -> 36.9 us  [shards(): gram, correlation = lax.psum((gram_local, correlation_local), ('occ', 'ao'))]
where the time goes in v1:
time: 263 us; the launch traced here: 262 us
  blocking collectives  82.5 us (31%)
  waiting for transfers between devices  76.1 us (29%)
  other arithmetic  46.9 us (18%)
  matrix products  28.4 us (11%)
  between operations  14.1 us (5%)
  local copies, waits for them, and re-layouts  13.6 us (5%)
    all_gather x1, waiting for transfers between devices, shards(): whole_rows = lax.all_gather(vir_coef, 'occ', axis=0, tiled=True)  75.4 us
    psum x2, blocking collectives, shards(): density = lax.psum(lax.psum(partial_value, 'ao'), 'occ')  45.6 us
    psum x1, blocking collectives, shards(): gram, correlation = lax.psum((gram_local, correlation_local), ('occ', 'ao'))  36.9 us
    reduce_sum x8, other arithmetic, gram_column(): jnp.sum(amplitudes.astype(jnp.float32) * sigma_one[None], axis=(1, 2))  34.4 us
    mul x8, local copies, waits for them, and re-layouts, gram_column(): amplitudes.astype(jnp.float32) * sigma_one[None]  12.1 us
    dot_general x1, matrix products, shards(): jnp.dot(amps_rows, amps_rows.T, preferred_element_type=jnp.float32)  11.1 us
    convert_element_type x1, other arithmetic, shards(): (sigma_block - ritz_values[:, None, None] * amplitudes.astype(jnp.float32...  10.8 us
    dot_general x1, matrix products, shards(): coupling = jnp.dot(weighted, whole_rows, preferred_element_type=jnp.float32)  9.7 us
  transfers between devices with their start and end apart: 1, of which 1 were waited for; matrix products, arithmetic and copies ran while one was open for 5% of the time, Pallas kernels for 0%

profile of v1, /device:TPU:0, one launch (start us, length us, event | category | flops | bytes accessed | tf_op | source)
XLA Modules:
  0.0 261.6 jit_solution(8905115315609625792)
XLA Ops:
  7.2 0.7 all-gather.2.cloned.1.call-update
  7.9 0.9 convert_bitcast_fusion
  8.8 11.1 %fusion.14 = f32[8,8]{1,0:T(8,128)S(1)} fusion(bf16[8,80,4864]{2,1,0:T(8,128)(2,1)} %param.8), kind=kOutput, calls=%fused_computation.17 | convolution fusion | flops 49807360 | bytes 6226176 | tf_op jit(solution)/shard_map/dot_general | solution.py:37
  19.9 0.2 broadcast_subtract_fusion
  20.1 75.4 %all-gather.2.cloned.1.call-done = bf16[512,4864]{1,0:T(8,128)(2,1)} async-done(((bf16[64,4864]{1,0:T(8,128)(2,1)}), bf16[512,4864]{1,0:T(8,128)(2,1)}) %all-gather.2.cloned.1.call-update) | async-done | bytes 4980752 | tf_op jit(solution)/shard_map/all_gather | solution.py:12
  95.5 7.6 %fusion.11 = f32[8,512]{1,0:T(8,128)S(1)} fusion(bf16[8,80,4864]{2,1,0:T(8,128)(2,1)} %param.8, bf16[512,4864]{1,0:T(8,128)(2,1)} %all-gather.2.cloned.1.call-done, f32[80,512]{1,0:T(8,128)S(1)} %convert_bitcast_fusion), kind=kOutput, calls=%fused_computation.16 | convolution fusion | flops 3188322304 | bytes 11386880 | tf_op jit(solution)/shard_map/dot_general | solution.py:14
  103.2 10.1 %psum.28 = f32[8,512]{1,0:T(8,128)S(1)} all-reduce(f32[8,512]{1,0:T(8,128)S(1)} %fusion.11), channel_id=1, replica_groups=mesh['occ'=8,'ao'=4] {'ao'}, use_global_device_ids=true, to_apply=%region_1.0 | all-reduce | flops 4096 | bytes 32768 | tf_op jit(solution)/shard_map/psum | solution.py:20
  113.3 35.5 %psum.29 = f32[8,512]{1,0:T(8,128)S(1)} all-reduce(f32[8,512]{1,0:T(8,128)S(1)} %psum.28), channel_id=1, replica_groups=mesh['occ'=8,'ao'=4] {'occ'}, use_global_device_ids=true, to_apply=%region_2.0 | all-reduce | flops 4096 | bytes 32768 | tf_op jit(solution)/shard_map/psum | solution.py:20
  148.8 9.7 %fusion = f32[8,80,4864]{2,1,0:T(8,128)} fusion(bf16[8,80,4864]{2,1,0:T(8,128)(2,1)} %param.8, f32[80,4864]{1,0:T(8,128)S(1)} %broadcast_subtract_fusion, bf16[512,4864]{1,0:T(8,128)(2,1)} %all-gather.2.cloned.1.call-done, f32[8,512]{1,0:T(8,128)S(1)} %broadcast_multiply_fusion, f32[80,512]{1,0:T(8,128)S(1)} %convert_bitcast_fusion), kind=kOutput, calls=%fused_computation.6 | convolution fusion | flops 3197665280 | bytes 25395200 | tf_op jit(solution)/shard_map/dot_general | solution.py:27
  158.5 46.7 %while.10 = (s32[]{:T(128)}, f32[8,8]{1,0:T(8,128)S(1)}, bf16[8,80,4864]{2,1,0:T(8,128)(2,1)}, f32[8,80,4864]{2,1,0:T(8,128)}, s32[]{:T(128)}, /*index=5*/s32[]{:T(128)}) while((s32[]{:T(128)}, f32[8,8]{1,0:T(8,128)S(1)}, bf16[8,80,4864]{2,1,0:T(8,128)(2,1)}, f32[8,80,4864]{2,1,0:T(8,128)}, s32[]{:T(128)}, /*index=5*/s32[]{:T(128)}) %tuple.23), condition=%wide.region_5.6_spmd, body=%wide.region_3.5_spmd.sunk | while | flops 9338874 | bytes 10895533 | solution.py:36
  158.5 1.5 dynamic-slice_bitcast_fusion.2
  160.0 4.3 %multiply_reduce_fusion.2 = f32[8]{0:T(128)S(1)} fusion(bf16[8,80,4864]{2,1,0:T(8,128)(2,1)} %get-tuple-element.76, f32[80,4864]{1,0:T(8,128)S(1)} %dynamic-slice_bitcast_fusion.2), kind=kLoop, calls=%fused_computation.2.clone.1 | loop fusion | flops 9338872 | bytes 7782432 | tf_op jit(solution)/shard_map/while/body/eval_jaxpr/reduce_sum | solution.py:34
  164.3 1.5 dynamic-slice_bitcast_fusion.2
  165.8 4.3 %multiply_reduce_fusion.2 = f32[8]{0:T(128)S(1)} fusion(bf16[8,80,4864]{2,1,0:T(8,128)(2,1)} %get-tuple-element.76, f32[80,4864]{1,0:T(8,128)S(1)} %dynamic-slice_bitcast_fusion.2), kind=kLoop, calls=%fused_computation.2.clone.1 | loop fusion | flops 9338872 | bytes 7782432 | tf_op jit(solution)/shard_map/while/body/eval_jaxpr/reduce_sum | solution.py:34
  170.1 1.5 dynamic-slice_bitcast_fusion.2
  171.6 4.3 %multiply_reduce_fusion.2 = f32[8]{0:T(128)S(1)} fusion(bf16[8,80,4864]{2,1,0:T(8,128)(2,1)} %get-tuple-element.76, f32[80,4864]{1,0:T(8,128)S(1)} %dynamic-slice_bitcast_fusion.2), kind=kLoop, calls=%fused_computation.2.clone.1 | loop fusion | flops 9338872 | bytes 7782432 | tf_op jit(solution)/shard_map/while/body/eval_jaxpr/reduce_sum | solution.py:34
  176.0 1.5 dynamic-slice_bitcast_fusion.2
  177.5 4.3 %multiply_reduce_fusion.2 = f32[8]{0:T(128)S(1)} fusion(bf16[8,80,4864]{2,1,0:T(8,128)(2,1)} %get-tuple-element.76, f32[80,4864]{1,0:T(8,128)S(1)} %dynamic-slice_bitcast_fusion.2), kind=kLoop, calls=%fused_computation.2.clone.1 | loop fusion | flops 9338872 | bytes 7782432 | tf_op jit(solution)/shard_map/while/body/eval_jaxpr/reduce_sum | solution.py:34
  181.8 1.5 dynamic-slice_bitcast_fusion.2
  183.3 4.3 %multiply_reduce_fusion.2 = f32[8]{0:T(128)S(1)} fusion(bf16[8,80,4864]{2,1,0:T(8,128)(2,1)} %get-tuple-element.76, f32[80,4864]{1,0:T(8,128)S(1)} %dynamic-slice_bitcast_fusion.2), kind=kLoop, calls=%fused_computation.2.clone.1 | loop fusion | flops 9338872 | bytes 7782432 | tf_op jit(solution)/shard_map/while/body/eval_jaxpr/reduce_sum | solution.py:34
  187.6 1.5 dynamic-slice_bitcast_fusion.2
  189.1 4.3 %multiply_reduce_fusion.2 = f32[8]{0:T(128)S(1)} fusion(bf16[8,80,4864]{2,1,0:T(8,128)(2,1)} %get-tuple-element.76, f32[80,4864]{1,0:T(8,128)S(1)} %dynamic-slice_bitcast_fusion.2), kind=kLoop, calls=%fused_computation.2.clone.1 | loop fusion | flops 9338872 | bytes 7782432 | tf_op jit(solution)/shard_map/while/body/eval_jaxpr/reduce_sum | solution.py:34
  193.5 1.5 dynamic-slice_bitcast_fusion.2
  195.0 4.3 %multiply_reduce_fusion.2 = f32[8]{0:T(128)S(1)} fusion(bf16[8,80,4864]{2,1,0:T(8,128)(2,1)} %get-tuple-element.76, f32[80,4864]{1,0:T(8,128)S(1)} %dynamic-slice_bitcast_fusion.2), kind=kLoop, calls=%fused_computation.2.clone.1 | loop fusion | flops 9338872 | bytes 7782432 | tf_op jit(solution)/shard_map/while/body/eval_jaxpr/reduce_sum | solution.py:34
  199.3 1.5 dynamic-slice_bitcast_fusion.2
  200.8 4.3 %multiply_reduce_fusion.2 = f32[8]{0:T(128)S(1)} fusion(bf16[8,80,4864]{2,1,0:T(8,128)(2,1)} %get-tuple-element.76, f32[80,4864]{1,0:T(8,128)S(1)} %dynamic-slice_bitcast_fusion.2), kind=kLoop, calls=%fused_computation.2.clone.1 | loop fusion | flops 9338872 | bytes 7782432 | tf_op jit(solution)/shard_map/while/body/eval_jaxpr/reduce_sum | solution.py:34
  205.1 0.1 copy.11
  205.2 36.9 %all-reduce = (f32[8,8]{1,0:T(8,128)S(1)}, f32[8,8]{1,0:T(8,128)S(1)}) all-reduce(f32[8,8]{1,0:T(8,128)S(1)} %bitcast.25, f32[8,8]{1,0:T(8,128)S(1)} %fusion.14), channel_id=1, replica_groups=mesh['occ'=8,'ao'=4] {'occ','ao'}, use_global_device_ids=true, to_apply=%region_6.7 | all-reduce | flops 128 | bytes 1024 | tf_op jit(solution)/shard_map/psum | solution.py:38
  242.1 0.6 gather_fusion
  242.7 0.6 gather_fusion.1
  243.4 0.7 rsqrt_multiply_fusion
  244.0 10.8 %fusion.2 = bf16[8,80,4864]{2,1,0:T(8,128)(2,1)} fusion(f32[8,80,4864]{2,1,0:T(8,128)} %get-tuple-element.82, bf16[8,80,4864]{2,1,0:T(8,128)(2,1)} %get-tuple-element.81, f32[8]{0:T(128)S(1)} %get-tuple-element.36), kind=kLoop, calls=%fused_computation.8 | loop fusion | flops 12451840 | bytes 24903712 | tf_op jit(solution)/shard_map/convert_element_type | solution.py:41
  (19 shorter events, 0.3 us)
Async XLA Ops:
  7.2 12.8 %copy-start.2 = (f32[80]{0:T(128)S(1)}, f32[80]{0:T(128)}, u32[]{:S(2)}) copy-start(f32[80]{0:T(128)} %param.11) | copy-start | bytes 964
  7.2 12.8 %copy-start = (f32[4864]{0:T(1024)S(1)}, f32[4864]{0:T(1024)}, u32[]{:S(2)}) copy-start(f32[4864]{0:T(1024)} %param.12) | copy-start | bytes 58372
  7.2 88.4 %all-gather.2.cloned.1.call-start = ((), (), s32[]{:S(2)}) async-start(), calls=%async_computation | async-start | bytes 5603328 | tf_op jit(solution)/shard_map/all_gather | solution.py:12
  20.1 128.6 %copy-start.1 = (f32[512]{0:T(512)S(1)}, f32[512]{0:T(512)}, u32[]{:S(2)}) copy-start(f32[512]{0:T(512)} %param.13) | copy-start | bytes 6148
Sparse Core Ops, SparseCore 0:
  10.2 85.3 all-gather.1
